TPU v7x, 32 devices: a whole 2x2x4 slice. The times are simulated.
32 devices in a mesh: sph: 8 (over z, core), rad: 4 (over y, x).
Axes of the slice: x: 2, y: 2, z: 4, core: 2. Of those that a mesh axis runs over, the one named last changes fastest.
Arguments:
- coeffs: bfloat16 [32768, 480], P('sph'), may hold values from -6 to 6
- interp: bfloat16 [32768, 2048], P('sph', 'rad'), may hold values from -0.06591797 to 0.06591797
- phases: float32 [64, 2048], P(None, 'rad'), may hold values from 0.3 to 3
- tables: bfloat16 [16, 480, 480], P('rad'), may hold values from -0.25 to 0.25
- bins: int32 [32768], P('sph'), may hold values from 0 to 63
Outputs:
- fields: bfloat16 [32768, 480], P('sph', 'rad')
All inputs are finite; a program needn't handle non-finite values.
Results may differ from a plain program's by a relative error of at most 0.024.
Values may be sent and summed in bfloat16 or wider, within the bound.
A program may use at most 64 MiB of HBM per device.

v0:
```python
import jax
import jax.numpy as jnp
from jax import lax
from jax.sharding import PartitionSpec as P


def body(coeffs, interp, phases, tables, bins):
    node_rows = interp.shape[1]
    onehot = (bins[:, None] == jnp.arange(phases.shape[0], dtype=jnp.int32)[None, :]).astype(
        jnp.float32
    )
    lifted = jnp.dot(
        onehot, phases, precision=lax.Precision.HIGHEST, preferred_element_type=jnp.float32
    )
    proj = (interp.astype(jnp.float32) * lifted).astype(jnp.bfloat16)
    partial_nodes = jnp.einsum("sr,sc->rc", proj, coeffs, preferred_element_type=jnp.float32)
    share = lax.psum_scatter(
        partial_nodes.astype(jnp.bfloat16), "sph", scatter_dimension=0, tiled=True
    ).astype(jnp.float32)
    rows = share.shape[0]
    first = lax.axis_index("sph") * rows
    which = first // (node_rows // tables.shape[0])
    table = lax.dynamic_index_in_dim(tables, which, 0, keepdims=False)
    local_part = jnp.dot(
        share.astype(jnp.bfloat16), table, preferred_element_type=jnp.float32
    ).astype(jnp.bfloat16)
    angular = lax.all_gather(local_part, "sph", axis=0, tiled=True)
    terms = jnp.dot(proj, angular, preferred_element_type=jnp.float32)
    fields = lax.psum_scatter(terms.astype(jnp.bfloat16), "rad", scatter_dimension=1, tiled=True)
    return fields


def solution(mesh):
    return jax.shard_map(
        body,
        mesh=mesh,
        in_specs=(P("sph", None), P("sph", "rad"), P(None, "rad"), P("rad", None, None), P("sph")),
        out_specs=P("sph", "rad"),
        check_vma=False,
    )
```

profile of v0, /device:TPU:0, one launch (start us, length us, event | category | flops | bytes accessed | tf_op | source)
XLA Modules:
  0.0 129.4 jit_solution(1361421610007537468)
XLA Ops:
  6.5 0.0 copy-start
  6.5 0.0 reduce-scatter.5.cloned.1.call-start
  6.5 0.0 copy-start.2
  6.5 5.6 %multiply_convert_fusion = bf16[4096,512]{1,0:T(8,128)(2,1)S(1)} fusion(bf16[4096,512]{1,0:T(8,128)(2,1)} %param.6, f32[64,512]{1,0:T(8,128)} %param.7, s32[4096]{0:T(1024)} %param.9), kind=kOutput, calls=%fused_computation | convolution fusion | flops 1617166336 | bytes 8536064 | tf_op jit(solution)/shard_map/dot_general | solution.py:12
  12.2 0.0 copy-start.1
  12.2 1.9 %copy-done.1 = bf16[4096,512]{1,0:T(8,128)(2,1)} copy-done((bf16[4096,512]{1,0:T(8,128)(2,1)}, bf16[4096,512]{1,0:T(8,128)(2,1)S(1)}, u32[]{:S(2)}) %copy-start.1) | copy-done | bytes 4194328
  14.1 0.0 copy-done.2
  14.1 3.2 %convolution_convert_fusion.1 = bf16[512,480]{1,0:T(8,128)(2,1)} fusion(bf16[4096,512]{1,0:T(8,128)(2,1)S(1)} %multiply_convert_fusion, bf16[4096,480]{0,1:T(8,128)(2,1)S(1)} %copy-done.2), kind=kOutput, calls=%fused_computation.3 | convolution fusion | flops 2013511680 | bytes 8617984 | tf_op jit(solution)/shard_map/sr,sc->rc/dot_general | solution.py:16
  17.3 0.0 reduce-scatter.5.cloned.1.call-update
  17.3 0.0 reduce-scatter.7.cloned.1.call-start
  17.4 34.0 %reduce-scatter.5.cloned.1.call-done = bf16[64,480]{1,0:T(8,128)(2,1)} async-done(((bf16[512,480]{1,0:T(8,128)(2,1)}), bf16[64,480]{1,0:T(8,128)(2,1)}) %reduce-scatter.5.cloned.1.call-update) | async-done | bytes 61456 | tf_op jit(solution)/shard_map/reduce_scatter | solution.py:17
  51.4 0.0 copy-done
  51.4 1.0 convolution_convert_fusion.2
  52.4 14.9 %all_gather.3 = bf16[512,480]{1,0:T(8,128)(2,1)S(1)} all-gather(bf16[64,480]{1,0:T(8,128)(2,1)S(1)} %convolution_convert_fusion.2), channel_id=1, replica_groups=mesh['sph'=8,'rad'=4] {'sph'}, dimensions={0}, use_global_device_ids=true | all-gather | bytes 552960 | tf_op jit(solution)/shard_map/all_gather | solution.py:27
  67.4 6.3 %convolution_convert_fusion = bf16[4096,480]{0,1:T(8,128)(2,1)} fusion(bf16[4096,512]{1,0:T(8,128)(2,1)} %copy-done.1, bf16[512,480]{1,0:T(8,128)(2,1)S(1)} %all_gather.3), kind=kOutput, calls=%fused_computation.1 | convolution fusion | flops 2015232000 | bytes 8617984 | tf_op jit(solution)/shard_map/dot_general | solution.py:28
  73.7 0.0 reduce-scatter.7.cloned.1.call-update
  73.7 48.9 %reduce-scatter.7.cloned.1.call-done = bf16[4096,120]{0,1:T(8,128)(2,1)} async-done(((bf16[4096,480]{0,1:T(8,128)(2,1)}), bf16[4096,120]{0,1:T(8,128)(2,1)}) %reduce-scatter.7.cloned.1.call-update) | async-done | bytes 983056
Async XLA Ops:
  6.5 44.8 %copy-start = (bf16[4,480,480]{2,1,0:T(8,128)(2,1)S(1)}, bf16[4,480,480]{2,1,0:T(8,128)(2,1)}, u32[]{:S(2)}) copy-start(bf16[4,480,480]{2,1,0:T(8,128)(2,1)} %param.8) | copy-start | bytes 5529604
  6.5 44.8 %reduce-scatter.5.cloned.1.call-start = ((), (), s32[]{:S(2)}) async-start(), calls=%async_computation.2 | async-start | bytes 589824 | tf_op jit(solution)/shard_map/reduce_scatter | solution.py:17
  6.5 7.6 %copy-start.2 = (bf16[4096,480]{0,1:T(8,128)(2,1)S(1)}, bf16[4096,480]{0,1:T(8,128)(2,1)}, u32[]{:S(2)}) copy-start(bf16[4096,480]{0,1:T(8,128)(2,1)} %param.5) | copy-start | bytes 11796484
  12.2 1.9 %copy-start.1 = (bf16[4096,512]{1,0:T(8,128)(2,1)}, bf16[4096,512]{1,0:T(8,128)(2,1)S(1)}, u32[]{:S(2)}) copy-start(bf16[4096,512]{1,0:T(8,128)(2,1)S(1)} %multiply_convert_fusion) | copy-start | bytes 12582916
  17.3 105.3 %reduce-scatter.7.cloned.1.call-start = ((), (), s32[]{:S(2)}) async-start(), calls=%async_computation.3 | async-start | bytes 4915200
Sparse Core Ops, SparseCore 0:
  17.5 33.8 reduce-scatter.4
  73.8 48.7 reduce-scatter.6
where the time goes:
time: 130 us; the launch traced here: 129 us
  waiting for transfers between devices  82.9 us (64%)
  matrix products  16.2 us (12%)
  blocking collectives  14.9 us (11%)
  between operations  13.4 us (10%)
  local copies, waits for them, and re-layouts  1.94 us (1%)
    unnamed x3, waiting for transfers between devices  48.9 us
    reduce_scatter x1, waiting for transfers between devices, body(): lax.psum_scatter(partial_nodes.astype(jnp.bfloat16), 'sph', scatter_dimen...  34 us
    all_gather x1, blocking collectives, body(): angular = lax.all_gather(local_part, 'sph', axis=0, tiled=True)  14.9 us
    dot_general x1, matrix products, body(): terms = jnp.dot(proj, angular, preferred_element_type=jnp.float32)  6.31 us
    dot_general x1, matrix products, body(): jnp.dot(onehot, phases, precision=lax.Precision.HIGHEST, preferred_elemen...  5.64 us
    dot_general x1, matrix products, body(): jnp.einsum('sr,sc->rc', proj, coeffs, preferred_element_type=jnp.float32)  3.18 us
  transfers between devices with their start and end apart: 2, of which 2 were waited for; matrix products, arithmetic and copies ran while one was open for 0% of the time, Pallas kernels for 0%

commit v1 on v0

v1 whole, which is shorter than its diff:
```python
import functools

import jax
import jax.numpy as jnp
from jax import lax
from jax.experimental import pallas as pl
from jax.experimental.pallas import tpu as pltpu
from jax.sharding import PartitionSpec as P

MESH = pl.DeviceIdType.MESH
F32, BF16 = jnp.float32, jnp.bfloat16


def plain_body(coeffs, interp, phases, tables, bins):
    node_rows = interp.shape[1]
    onehot = (bins[:, None] == jnp.arange(phases.shape[0], dtype=jnp.int32)[None, :]).astype(F32)
    lifted = jnp.dot(onehot, phases, precision=lax.Precision.HIGHEST, preferred_element_type=F32)
    proj = (interp.astype(F32) * lifted).astype(BF16)
    partial_nodes = jnp.einsum("sr,sc->rc", proj, coeffs, preferred_element_type=F32)
    share = lax.psum_scatter(partial_nodes.astype(BF16), "sph", scatter_dimension=0, tiled=True)
    rows = share.shape[0]
    which = lax.axis_index("sph") * rows // (node_rows // tables.shape[0])
    table = lax.dynamic_index_in_dim(tables, which, 0, keepdims=False)
    local_part = jnp.dot(share, table, preferred_element_type=F32).astype(BF16)
    angular = lax.all_gather(local_part, "sph", axis=0, tiled=True)
    terms = jnp.dot(proj, angular, preferred_element_type=F32)
    return lax.psum_scatter(terms.astype(BF16), "rad", scatter_dimension=1, tiled=True)


def kernel(
    n_sph, n_chunks,
    coeffs_hbm, interp_hbm, phases_ref, tables_hbm, bins_ref, out_ref,
    coeffs, interp, table, lift_w, projt, acc,
    pair_out, pair_in, line_out, line_in, ang, angt,
    s1_out, s1_in, s2_out, s2_in, keep,
    load_sem, table_sem, pair_sem, line_sem, gather_sem, relay_sem, s1_sem, s2_sem,
):
    sph, rad = lax.axis_index("sph"), lax.axis_index("rad")
    n_z = n_sph // 2
    z, core = sph // 2, sph % 2
    y, x = rad // 2, rad % 2
    other_core = z * 2 + 1 - core
    across_x, across_y = y * 2 + 1 - x, (1 - y) * 2 + x
    chunk = projt.shape[2]
    nodes, cols = projt.shape[1], coeffs.shape[2]
    rows = acc.shape[1]
    block = cols // 4
    half = n_chunks // 2

    def along(d):
        return ((z + d) % n_z) * 2 + core

    def origin(d):
        return (z + n_z - d) % n_z

    def loads(k):
        at = pl.ds(k * chunk, chunk)
        return (
            pltpu.make_async_copy(interp_hbm.at[at], interp.at[k], load_sem.at[0, k]),
            pltpu.make_async_copy(coeffs_hbm.at[at], coeffs.at[k], load_sem.at[1, k]),
        )

    for k in range(n_chunks):
        for copy in loads(k):
            copy.start()
    which = sph * rows // (nodes // tables_hbm.shape[0])
    table_copy = pltpu.make_async_copy(tables_hbm.at[which], table, table_sem)
    table_copy.start()

    barrier = pltpu.get_barrier_semaphore()
    partners = [(other_core, rad)] + [(along(d), rad) for d in range(1, n_z)]
    partners += [(sph, across_x), (sph, across_y)]
    for partner in partners:
        pl.semaphore_signal(barrier, inc=1, device_id=partner, device_id_type=MESH)

    whole = phases_ref[...]
    hi = whole.astype(BF16).astype(F32)
    mid = (whole - hi).astype(BF16).astype(F32)
    lo = (whole - hi) - mid
    parts = jnp.concatenate([hi, mid, lo, jnp.zeros_like(hi)], axis=0)
    lift_w[...] = parts.T.astype(BF16)
    acc[...] = jnp.zeros_like(acc)

    def project(k, carry):
        a, b = loads(k)
        a.wait()
        here = bins_ref[k]
        level = lax.broadcasted_iota(jnp.int32, (whole.shape[0], chunk), 0)
        hot = jnp.where(level == here, 1.0, 0.0).astype(BF16)
        lifted = jnp.dot(lift_w[...], jnp.concatenate([hot] * 4, axis=0), preferred_element_type=F32)
        projt[k] = (interp[k].T.astype(F32) * lifted).astype(BF16)
        b.wait()
        acc[...] += jnp.dot(projt[k], coeffs[k], preferred_element_type=F32).reshape(acc.shape)
        return carry

    lax.fori_loop(0, n_chunks, project, 0)

    for i in range(n_z):
        pair_out[i] = acc[2 * i + 1 - core].astype(BF16)
    pl.semaphore_wait(barrier, len(partners))

    def remote(src, dst, sems, at, device):
        return pltpu.make_async_remote_copy(
            src_ref=src, dst_ref=dst, send_sem=sems.at[(0, *at)], recv_sem=sems.at[(1, *at)],
            device_id=device, device_id_type=MESH,
        )

    pair = remote(pair_out, pair_in, pair_sem, (), (other_core, rad))
    pair.start()
    pair.wait_recv()
    sends = [
        remote(line_out.at[d - 1], line_in.at[d - 1], line_sem, (d - 1,), (along(d), rad))
        for d in range(1, n_z)
    ]
    for d in range(n_z - 1, 0, -1):
        to = (z + d) % n_z
        line_out[d - 1] = (acc[2 * to + core] + pair_in[to].astype(F32)).astype(BF16)
        sends[d - 1].start()
    total = acc[sph] + pair_in[z].astype(F32)
    for d in range(1, n_z):
        sends[d - 1].wait_recv()
        total = total + line_in[d - 1].astype(F32)
    table_copy.wait()
    ang[sph] = jnp.dot(total.astype(BF16), table[...], preferred_element_type=F32).astype(BF16)

    gathers = [
        remote(ang.at[sph], ang.at[sph], gather_sem, (d - 1,), (along(d), rad)) for d in range(1, n_z)
    ]
    relays = []
    for d in range(n_z):
        piece = ang.at[origin(d) * 2 + core]
        relays.append(remote(piece, piece, relay_sem, (d,), (other_core, rad)))
    for d in range(n_z - 1, 0, -1):
        gathers[d - 1].start()
    relays[0].start()
    for d in range(1, n_z):
        gathers[d - 1].wait_recv()
        relays[d].start()
    for d in range(n_z):
        relays[d].wait_recv()

    turned = ang[...].reshape(nodes, cols).astype(F32).T
    q = [turned[i * block:(i + 1) * block] for i in range(4)]
    for h, g, first, second in ((0, 0, 0, 2), (0, 1, 1, 3), (1, 0, 0, 1), (1, 1, 2, 3)):
        angt[h, g] = jnp.concatenate([q[first], q[second]], axis=0).astype(BF16)

    side = (x, y)
    first_to, second_to = (across_x, across_y), (across_y, across_x)

    def stage1(h, k):
        return remote(s1_out.at[h, k], s1_in.at[h, k], s1_sem, (h, k), (sph, first_to[h]))

    def stage2(h, k):
        return remote(s2_out.at[h, k], s2_in.at[h, k], s2_sem, (h, k), (sph, second_to[h]))

    def give(k, carry):
        for h in range(2):
            s1_out[h, k] = jnp.dot(
                angt[h, 1 - side[h]], projt[h * half + k], preferred_element_type=F32
            ).astype(BF16)
            stage1(h, k).start()
        return carry

    lax.fori_loop(0, half, give, 0)

    def join(k, carry):
        for h in range(2):
            mine = jnp.dot(angt[h, side[h]], projt[h * half + k], preferred_element_type=F32)
            stage1(h, k).wait_recv()
            mine = mine + s1_in[h, k].astype(F32)
            low, high = mine[:block], mine[block:]
            lower = side[1 - h] == 0
            keep[h, k] = jnp.where(lower, low, high)
            away = jnp.where(lower, high, low)
            s2_out[h, k] = jnp.concatenate([away[:, :chunk // 2], away[:, chunk // 2:]], axis=0).astype(BF16)
            stage2(h, k).start()
        return carry

    lax.fori_loop(0, half, join, 0)

    def finish(k, carry):
        for h in range(2):
            stage2(h, k).wait_recv()
            got = s2_in[h, k].astype(F32)
            field = keep[h, k] + jnp.concatenate([got[:block], got[block:]], axis=1)
            out_ref[pl.ds(pl.multiple_of((h * half + k) * chunk, chunk), chunk)] = field.T.astype(BF16)
        return carry

    lax.fori_loop(0, half, finish, 0)

    pair.wait_send()
    for copy in sends + gathers + relays:
        copy.wait_send()

    def drain(k, carry):
        for h in range(2):
            stage1(h, k).wait_send()
            stage2(h, k).wait_send()
        return carry

    lax.fori_loop(0, half, drain, 0)


def fused_body(n_sph, n_rad, chunk, coeffs, interp, phases, tables, bins):
    spheres, nodes = interp.shape
    cols = coeffs.shape[1]
    n_chunks = spheres // chunk
    half, rows, n_z, block = n_chunks // 2, nodes // n_sph, n_sph // 2, cols // n_rad
    levels = phases.shape[0]
    vmem = pl.BlockSpec(memory_space=pltpu.VMEM)
    hbm = pl.BlockSpec(memory_space=pl.ANY)
    dma = pltpu.SemaphoreType.DMA
    return pl.pallas_call(
        functools.partial(kernel, n_sph, n_chunks),
        out_shape=jax.ShapeDtypeStruct((spheres, block), BF16),
        in_specs=[hbm, hbm, vmem, hbm, vmem],
        out_specs=vmem,
        scratch_shapes=[
            pltpu.VMEM((n_chunks, chunk, cols), BF16),
            pltpu.VMEM((n_chunks, chunk, nodes), BF16),
            pltpu.VMEM((cols, cols), BF16),
            pltpu.VMEM((nodes, 4 * levels), BF16),
            pltpu.VMEM((n_chunks, nodes, chunk), BF16),
            pltpu.VMEM((n_sph, rows, cols), F32),
            pltpu.VMEM((n_z, rows, cols), BF16),
            pltpu.VMEM((n_z, rows, cols), BF16),
            pltpu.VMEM((n_z - 1, rows, cols), BF16),
            pltpu.VMEM((n_z - 1, rows, cols), BF16),
            pltpu.VMEM((n_sph, rows, cols), BF16),
            pltpu.VMEM((2, 2, 2 * block, nodes), BF16),
            pltpu.VMEM((2, half, 2 * block, chunk), BF16),
            pltpu.VMEM((2, half, 2 * block, chunk), BF16),
            pltpu.VMEM((2, half, 2 * block, chunk // 2), BF16),
            pltpu.VMEM((2, half, 2 * block, chunk // 2), BF16),
            pltpu.VMEM((2, half, block, chunk), F32),
            dma((2, n_chunks)),
            dma,
            dma((2,)),
            dma((2, n_z - 1)),
            dma((2, n_z - 1)),
            dma((2, n_z)),
            dma((2, 2, half)),
            dma((2, 2, half)),
        ],
        compiler_params=pltpu.CompilerParams(
            collective_id=0, has_side_effects=True, vmem_limit_bytes=60 * 1024 * 1024
        ),
    )(coeffs, interp, phases, tables, bins.reshape(n_chunks, 1, chunk))


def solution(mesh):
    n_sph, n_rad = mesh.shape["sph"], mesh.shape["rad"]

    def body(coeffs, interp, phases, tables, bins):
        spheres, nodes = interp.shape
        chunk = spheres // 8
        fits = (
            n_rad == 4
            and n_sph % 2 == 0
            and n_sph >= 4
            and coeffs.shape[1] % (8 * n_rad) == 0
            and nodes % (16 * n_sph) == 0
            and (nodes // tables.shape[0]) % (nodes // n_sph) == 0
            and spheres % 8 == 0
            and chunk % 256 == 0
        )
        if fits:
            return fused_body(n_sph, n_rad, chunk, coeffs, interp, phases, tables, bins)
        return plain_body(coeffs, interp, phases, tables, bins)

    return jax.shard_map(
        body,
        mesh=mesh,
        in_specs=(P("sph", None), P("sph", "rad"), P(None, "rad"), P("rad", None, None), P("sph")),
        out_specs=P("sph", "rad"),
        check_vma=False,
    )
```

time: 130 us -> 73.9 us (0.57)
  waiting for transfers between devices: 82.9 us -> 0 us
  Pallas kernels: 0 us -> 64.9 us
  matrix products: 16.2 us -> 0 us
  blocking collectives: 14.9 us -> 0 us
  between operations: 13.4 us -> 0.01 us
  local copies, waits for them, and re-layouts: 1.94 us -> 8.68 us
    pallas_call x0 -> x1, Pallas kernels: none -> 64.9 us  [fused_body(): pl.pallas_call(functools.partial(kernel, n_sph, n_chunks), out_shape=jax....]
    unnamed x3 -> x0, waiting for transfers between devices: 48.9 us -> none
    reduce_scatter x1 -> x0, waiting for transfers between devices: 34 us -> none  [body(): lax.psum_scatter(partial_nodes.astype(jnp.bfloat16), 'sph', scatter_dimen...]
    dot_general x4 -> x0, matrix products: 16.2 us -> none  [the longest x1 6.31 us: body(): terms = jnp.dot(proj, angular, preferred_element_type=jnp.float32)]
    all_gather x1 -> x0, blocking collectives: 14.9 us -> none  [body(): angular = lax.all_gather(local_part, 'sph', axis=0, tiled=True)]
    unnamed x6 -> x1, local copies, waits for them, and re-layouts: 1.94 us -> 6.44 us
    pallas_call x0 -> x1, local copies, waits for them, and re-layouts: none -> 2.25 us  [fused_body(): pl.pallas_call(functools.partial(kernel, n_sph, n_chunks), out_shape=jax....]
  transfers between devices with their start and end apart: 2 -> 0, of which waited for: 2 -> 0; matrix products, arithmetic and copies ran while one was open for 0% -> 0% of each run, Pallas kernels for 0% -> 0%
where the time goes in v1:
time: 73.9 us; the launch traced here: 73.6 us
  Pallas kernels  64.9 us (88%)
  local copies, waits for them, and re-layouts  8.68 us (12%)
    pallas_call x1, Pallas kernels, fused_body(): pl.pallas_call(functools.partial(kernel, n_sph, n_chunks), out_shape=jax....  64.9 us
    unnamed x1, local copies, waits for them, and re-layouts  6.44 us
    pallas_call x1, local copies, waits for them, and re-layouts, fused_body(): pl.pallas_call(functools.partial(kernel, n_sph, n_chunks), out_shape=jax....  2.25 us

profile of v1, /device:TPU:0, one launch (start us, length us, event | category | flops | bytes accessed | tf_op | source)
XLA Modules:
  0.0 73.6 jit_solution(10651299876348930894)
XLA Ops:
  0.0 6.4 %copy.6.coeffs_hbm = bf16[4096,480]{1,0:T(8,128)(2,1)} copy(bf16[4096,480]{0,1:T(8,128)(2,1)} %param.5) | data formatting | bytes 7864320 | tf_op args[0]
  6.4 64.9 %shard_map.55 = bf16[4096,120]{1,0:T(8,128)(2,1)} custom-call(bf16[4096,480]{1,0:T(8,128)(2,1)} %copy.6.coeffs_hbm, bf16[4096,512]{1,0:T(8,128)(2,1)} %interp_hbm.1, f32[64,512]{1,0:T(8,128)} %phases_ref.1, bf16[4,480,480]{2,1,0:T(8,128)(2,1)} %tables_hbm.1, s32[8,1,512]{2,1,0:T(1,128)} %bitcast.1), custom_call_target="tpu_custom_call" | custom-call | tf_op jit(solution)/shard_map/pallas_call | solution.py:213
  71.4 2.2 %copy.7 = bf16[4096,120]{0,1:T(8,128)(2,1)} copy(bf16[4096,120]{1,0:T(8,128)(2,1)} %shard_map.55) | data formatting | bytes 1966080 | tf_op jit(solution)/shard_map/pallas_call | solution.py:213

commit v2 on v1

--- a/solution.py
+++ b/solution.py
@@ -31,9 +31,8 @@
     n_sph, n_chunks,
     coeffs_hbm, interp_hbm, phases_ref, tables_hbm, bins_ref, out_ref,
     coeffs, interp, table, lift_w, projt, acc,
-    pair_out, pair_in, line_out, line_in, ang, angt,
-    s1_out, s1_in, s2_out, s2_in, keep,
-    load_sem, table_sem, pair_sem, line_sem, gather_sem, relay_sem, s1_sem, s2_sem,
+    pair_out, pair_in, line_out, line_in, ang, angt, sent, got,
+    load_sem, table_sem, pair_sem, line_sem, gather_sem, relay_sem, field_sem,
 ):
     sph, rad = lax.axis_index("sph"), lax.axis_index("rad")
     n_z = n_sph // 2
@@ -42,7 +41,7 @@
     other_core = z * 2 + 1 - core
     across_x, across_y = y * 2 + 1 - x, (1 - y) * 2 + x
     chunk = projt.shape[2]
-    nodes, cols = projt.shape[1], coeffs.shape[2]
+    nodes, cols = projt.shape[1], coeffs.shape[1]
     rows = acc.shape[1]
     block = cols // 4
     half = n_chunks // 2
@@ -57,7 +56,7 @@
         at = pl.ds(k * chunk, chunk)
         return (
             pltpu.make_async_copy(interp_hbm.at[at], interp.at[k], load_sem.at[0, k]),
-            pltpu.make_async_copy(coeffs_hbm.at[at], coeffs.at[k], load_sem.at[1, k]),
+            pltpu.make_async_copy(coeffs_hbm.at[:, at], coeffs.at[k], load_sem.at[1, k]),
         )
 
     for k in range(n_chunks):
@@ -90,7 +89,9 @@
         lifted = jnp.dot(lift_w[...], jnp.concatenate([hot] * 4, axis=0), preferred_element_type=F32)
         projt[k] = (interp[k].T.astype(F32) * lifted).astype(BF16)
         b.wait()
-        acc[...] += jnp.dot(projt[k], coeffs[k], preferred_element_type=F32).reshape(acc.shape)
+        acc[...] += lax.dot_general(
+            projt[k], coeffs[k], (((1,), (1,)), ((), ())), preferred_element_type=F32
+        ).reshape(acc.shape)
         return carry
 
     lax.fori_loop(0, n_chunks, project, 0)
@@ -104,6 +105,14 @@
             src_ref=src, dst_ref=dst, send_sem=sems.at[(0, *at)], recv_sem=sems.at[(1, *at)],
             device_id=device, device_id_type=MESH,
         )
+
+    def gather(p, d):
+        mine = ang.at[p, sph, pl.ds(0, 1 + 2 * p)]
+        return remote(mine, mine, gather_sem, (p, d - 1), (along(d), rad))
+
+    def relay(p, d):
+        piece = ang.at[p, origin(d) * 2 + core, pl.ds(0, 1 + 2 * p)]
+        return remote(piece, piece, relay_sem, (p, d), (other_core, rad))
 
     pair = remote(pair_out, pair_in, pair_sem, (), (other_core, rad))
     pair.start()
@@ -121,81 +130,96 @@
         sends[d - 1].wait_recv()
         total = total + line_in[d - 1].astype(F32)
     table_copy.wait()
-    ang[sph] = jnp.dot(total.astype(BF16), table[...], preferred_element_type=F32).astype(BF16)
-
-    gathers = [
-        remote(ang.at[sph], ang.at[sph], gather_sem, (d - 1,), (along(d), rad)) for d in range(1, n_z)
-    ]
-    relays = []
-    for d in range(n_z):
-        piece = ang.at[origin(d) * 2 + core]
-        relays.append(remote(piece, piece, relay_sem, (d,), (other_core, rad)))
-    for d in range(n_z - 1, 0, -1):
-        gathers[d - 1].start()
-    relays[0].start()
-    for d in range(1, n_z):
-        gathers[d - 1].wait_recv()
-        relays[d].start()
-    for d in range(n_z):
-        relays[d].wait_recv()
-
-    turned = ang[...].reshape(nodes, cols).astype(F32).T
-    q = [turned[i * block:(i + 1) * block] for i in range(4)]
-    for h, g, first, second in ((0, 0, 0, 2), (0, 1, 1, 3), (1, 0, 0, 1), (1, 1, 2, 3)):
-        angt[h, g] = jnp.concatenate([q[first], q[second]], axis=0).astype(BF16)
-
-    side = (x, y)
+    share = jnp.dot(total.astype(BF16), table[...], preferred_element_type=F32)
+    q = [share[:, i * block:(i + 1) * block] for i in range(4)]
+    far_row = [jnp.where(y == 0, q[2 + i], q[i]) for i in range(2)]
+    near_row = [jnp.where(y == 0, q[i], q[2 + i]) for i in range(2)]
+    diagonal = jnp.where(x == 0, far_row[1], far_row[0])
+    same_x = jnp.where(x == 0, far_row[0], far_row[1])
+    same_y = jnp.where(x == 0, near_row[1], near_row[0])
+    own = jnp.where(x == 0, near_row[0], near_row[1])
+    for i, part in enumerate((diagonal, same_x, same_y, own)):
+        ang[min(i, 1), sph, max(i - 1, 0)] = part.astype(BF16)
+        if i == 0 or i == 3:
+            p = min(i, 1)
+            for d in range(n_z - 1, 0, -1):
+                gather(p, d).start()
+            relay(p, 0).start()
+
+    def collect(p):
+        for d in range(1, n_z):
+            gather(p, d).wait_recv()
+            relay(p, d).start()
+        for d in range(n_z):
+            relay(p, d).wait_recv()
+
     first_to, second_to = (across_x, across_y), (across_y, across_x)
 
-    def stage1(h, k):
-        return remote(s1_out.at[h, k], s1_in.at[h, k], s1_sem, (h, k), (sph, first_to[h]))
-
-    def stage2(h, k):
-        return remote(s2_out.at[h, k], s2_in.at[h, k], s2_sem, (h, k), (sph, second_to[h]))
+    def field(stage, h, k):
+        to = second_to[h] if stage == 1 else first_to[h]
+        return remote(sent.at[stage, h, k], got.at[stage, h, k], field_sem, (stage, h, k), (sph, to))
+
+    def terms(i, h, k):
+        return jnp.dot(angt[i], projt[h * half + k], preferred_element_type=F32)
+
+    def pack(v):
+        return jnp.concatenate([v[:, :chunk // 2], v[:, chunk // 2:]], axis=0).astype(BF16)
+
+    def unpack(v):
+        v = v.astype(F32)
+        return jnp.concatenate([v[:block], v[block:]], axis=1)
+
+    collect(0)
+    angt[0] = ang[0, :, 0].reshape(nodes, block).astype(F32).T.astype(BF16)
 
     def give(k, carry):
         for h in range(2):
-            s1_out[h, k] = jnp.dot(
-                angt[h, 1 - side[h]], projt[h * half + k], preferred_element_type=F32
-            ).astype(BF16)
-            stage1(h, k).start()
+            sent[0, h, k] = pack(terms(0, h, k))
+            field(0, h, k).start()
         return carry
 
     lax.fori_loop(0, half, give, 0)
 
+    collect(1)
+    for i in range(3):
+        angt[1 + i] = ang[1, :, i].reshape(nodes, block).astype(F32).T.astype(BF16)
+
     def join(k, carry):
         for h in range(2):
-            mine = jnp.dot(angt[h, side[h]], projt[h * half + k], preferred_element_type=F32)
-            stage1(h, k).wait_recv()
-            mine = mine + s1_in[h, k].astype(F32)
-            low, high = mine[:block], mine[block:]
-            lower = side[1 - h] == 0
-            keep[h, k] = jnp.where(lower, low, high)
-            away = jnp.where(lower, high, low)
-            s2_out[h, k] = jnp.concatenate([away[:, :chunk // 2], away[:, chunk // 2:]], axis=0).astype(BF16)
-            stage2(h, k).start()
+            sent[2, h, k] = pack(terms(2 - h, h, k))
+            mine = terms(1 + h, h, k)
+            field(0, h, k).wait_recv()
+            sent[1, h, k] = pack(mine + unpack(got[0, h, k]))
+            field(1, h, k).start()
+            field(2, h, k).start()
         return carry
 
     lax.fori_loop(0, half, join, 0)
 
     def finish(k, carry):
         for h in range(2):
-            stage2(h, k).wait_recv()
-            got = s2_in[h, k].astype(F32)
-            field = keep[h, k] + jnp.concatenate([got[:block], got[block:]], axis=1)
-            out_ref[pl.ds(pl.multiple_of((h * half + k) * chunk, chunk), chunk)] = field.T.astype(BF16)
+            mine = terms(3, h, k)
+            field(1, h, k).wait_recv()
+            field(2, h, k).wait_recv()
+            mine = mine + unpack(got[1, h, k]) + unpack(got[2, h, k])
+            out_ref[:, pl.ds(pl.multiple_of((h * half + k) * chunk, chunk), chunk)] = mine.astype(BF16)
         return carry
 
     lax.fori_loop(0, half, finish, 0)
 
     pair.wait_send()
-    for copy in sends + gathers + relays:
+    for copy in sends:
         copy.wait_send()
+    for p in range(2):
+        for d in range(1, n_z):
+            gather(p, d).wait_send()
+        for d in range(n_z):
+            relay(p, d).wait_send()
 
     def drain(k, carry):
         for h in range(2):
-            stage1(h, k).wait_send()
-            stage2(h, k).wait_send()
+            for stage in range(3):
+                field(stage, h, k).wait_send()
         return carry
 
     lax.fori_loop(0, half, drain, 0)
@@ -212,11 +236,11 @@
     dma = pltpu.SemaphoreType.DMA
     return pl.pallas_call(
         functools.partial(kernel, n_sph, n_chunks),
-        out_shape=jax.ShapeDtypeStruct((spheres, block), BF16),
+        out_shape=jax.ShapeDtypeStruct((block, spheres), BF16),
         in_specs=[hbm, hbm, vmem, hbm, vmem],
         out_specs=vmem,
         scratch_shapes=[
-            pltpu.VMEM((n_chunks, chunk, cols), BF16),
+            pltpu.VMEM((n_chunks, cols, chunk), BF16),
             pltpu.VMEM((n_chunks, chunk, nodes), BF16),
             pltpu.VMEM((cols, cols), BF16),
             pltpu.VMEM((nodes, 4 * levels), BF16),
@@ -226,26 +250,22 @@
             pltpu.VMEM((n_z, rows, cols), BF16),
             pltpu.VMEM((n_z - 1, rows, cols), BF16),
             pltpu.VMEM((n_z - 1, rows, cols), BF16),
-            pltpu.VMEM((n_sph, rows, cols), BF16),
-            pltpu.VMEM((2, 2, 2 * block, nodes), BF16),
-            pltpu.VMEM((2, half, 2 * block, chunk), BF16),
-            pltpu.VMEM((2, half, 2 * block, chunk), BF16),
-            pltpu.VMEM((2, half, 2 * block, chunk // 2), BF16),
-            pltpu.VMEM((2, half, 2 * block, chunk // 2), BF16),
-            pltpu.VMEM((2, half, block, chunk), F32),
+            pltpu.VMEM((2, n_sph, 3, rows, block), BF16),
+            pltpu.VMEM((4, block, nodes), BF16),
+            pltpu.VMEM((3, 2, half, 2 * block, chunk // 2), BF16),
+            pltpu.VMEM((3, 2, half, 2 * block, chunk // 2), BF16),
             dma((2, n_chunks)),
             dma,
             dma((2,)),
             dma((2, n_z - 1)),
-            dma((2, n_z - 1)),
-            dma((2, n_z)),
-            dma((2, 2, half)),
-            dma((2, 2, half)),
+            dma((2, 2, n_z - 1)),
+            dma((2, 2, n_z)),
+            dma((2, 3, 2, half)),
         ],
         compiler_params=pltpu.CompilerParams(
             collective_id=0, has_side_effects=True, vmem_limit_bytes=60 * 1024 * 1024
         ),
-    )(coeffs, interp, phases, tables, bins.reshape(n_chunks, 1, chunk))
+    )(coeffs.T, interp, phases, tables, bins.reshape(n_chunks, 1, chunk)).T
 
 
 def solution(mesh):

time: 73.9 us -> 63.4 us (0.86)
  local copies, waits for them, and re-layouts: 8.68 us -> 2.23 us
  Pallas kernels: 64.9 us -> 61 us
    unnamed x1, local copies, waits for them, and re-layouts: 6.44 us -> 2.23 us
    pallas_call x1, Pallas kernels: 64.9 us -> 61 us  [fused_body(): pl.pallas_call(functools.partial(kernel, n_sph, n_chunks), out_shape=jax....]
    pallas_call x1 -> x0, local copies, waits for them, and re-layouts: 2.25 us -> none  [fused_body(): pl.pallas_call(functools.partial(kernel, n_sph, n_chunks), out_shape=jax....]
where the time goes in v2:
time: 63.4 us; the launch traced here: 63.3 us
  Pallas kernels  61 us (96%)
  local copies, waits for them, and re-layouts  2.23 us (4%)
    pallas_call x1, Pallas kernels, fused_body(): pl.pallas_call(functools.partial(kernel, n_sph, n_chunks), out_shape=jax....  61 us
    unnamed x1, local copies, waits for them, and re-layouts  2.23 us

profile of v2, /device:TPU:0, one launch (start us, length us, event | category | flops | bytes accessed | tf_op | source)
XLA Modules:
  0.0 63.3 jit_solution(13795737096918168744)
XLA Ops:
  0.0 61.0 %shard_map.55 = bf16[120,4096]{1,0:T(8,128)(2,1)} custom-call(bf16[480,4096]{1,0:T(8,128)(2,1)} %bitcast.3, bf16[4096,512]{1,0:T(8,128)(2,1)} %interp_hbm.1, f32[64,512]{1,0:T(8,128)} %phases_ref.1, bf16[4,480,480]{2,1,0:T(8,128)(2,1)} %tables_hbm.1, s32[8,1,512]{2,1,0:T(1,128)} %bitcast.5), custom_call_target="tpu_custom_call" | custom-call | tf_op jit(solution)/shard_map/pallas_call | solution.py:237
  61.0 2.2 %copy.7 = bf16[4096,120]{0,1:T(8,128)(2,1)} copy(bf16[4096,120]{0,1:T(8,128)(2,1)} %bitcast.4) | data formatting | bytes 1966080

commit v3 on v2

--- a/solution.py
+++ b/solution.py
@@ -96,8 +96,6 @@
 
     lax.fori_loop(0, n_chunks, project, 0)
 
-    for i in range(n_z):
-        pair_out[i] = acc[2 * i + 1 - core].astype(BF16)
     pl.semaphore_wait(barrier, len(partners))
 
     def remote(src, dst, sems, at, device):
@@ -114,18 +112,23 @@
         piece = ang.at[p, origin(d) * 2 + core, pl.ds(0, 1 + 2 * p)]
         return remote(piece, piece, relay_sem, (p, d), (other_core, rad))
 
-    pair = remote(pair_out, pair_in, pair_sem, (), (other_core, rad))
-    pair.start()
-    pair.wait_recv()
+    pairs = [
+        remote(pair_out.at[d], pair_in.at[d], pair_sem, (d,), (other_core, rad)) for d in range(n_z)
+    ]
+    for d in range(n_z - 1, -1, -1):
+        pair_out[d] = acc[2 * ((z + d) % n_z) + 1 - core].astype(BF16)
+        pairs[d].start()
     sends = [
         remote(line_out.at[d - 1], line_in.at[d - 1], line_sem, (d - 1,), (along(d), rad))
         for d in range(1, n_z)
     ]
     for d in range(n_z - 1, 0, -1):
         to = (z + d) % n_z
-        line_out[d - 1] = (acc[2 * to + core] + pair_in[to].astype(F32)).astype(BF16)
+        pairs[d].wait_recv()
+        line_out[d - 1] = (acc[2 * to + core] + pair_in[d].astype(F32)).astype(BF16)
         sends[d - 1].start()
-    total = acc[sph] + pair_in[z].astype(F32)
+    pairs[0].wait_recv()
+    total = acc[sph] + pair_in[0].astype(F32)
     for d in range(1, n_z):
         sends[d - 1].wait_recv()
         total = total + line_in[d - 1].astype(F32)
@@ -207,8 +210,7 @@
 
     lax.fori_loop(0, half, finish, 0)
 
-    pair.wait_send()
-    for copy in sends:
+    for copy in pairs + sends:
         copy.wait_send()
     for p in range(2):
         for d in range(1, n_z):
@@ -236,7 +238,7 @@
     dma = pltpu.SemaphoreType.DMA
     return pl.pallas_call(
         functools.partial(kernel, n_sph, n_chunks),
-        out_shape=jax.ShapeDtypeStruct((block, spheres), BF16),
+        out_shape=pltpu.VMEM((block, spheres), BF16),
         in_specs=[hbm, hbm, vmem, hbm, vmem],
         out_specs=vmem,
         scratch_shapes=[
@@ -256,7 +258,7 @@
             pltpu.VMEM((3, 2, half, 2 * block, chunk // 2), BF16),
             dma((2, n_chunks)),
             dma,
-            dma((2,)),
+            dma((2, n_z)),
             dma((2, n_z - 1)),
             dma((2, 2, n_z - 1)),
             dma((2, 2, n_z)),

time: 63.4 us -> 60.9 us (0.961)
  local copies, waits for them, and re-layouts: 2.23 us -> 0.95 us
  Pallas kernels: 61 us -> 59.8 us
    unnamed x1, local copies, waits for them, and re-layouts: 2.23 us -> 0.95 us
    pallas_call x1, Pallas kernels: 61 us -> 59.8 us  [fused_body(): pl.pallas_call(functools.partial(kernel, n_sph, n_chunks), out_shape=pltp...]
where the time goes in v3:
time: 60.9 us; the launch traced here: 60.8 us
  Pallas kernels  59.8 us (98%)
  local copies, waits for them, and re-layouts  0.95 us (2%)
    pallas_call x1, Pallas kernels, fused_body(): pl.pallas_call(functools.partial(kernel, n_sph, n_chunks), out_shape=pltp...  59.8 us

profile of v3, /device:TPU:0, one launch (start us, length us, event | category | flops | bytes accessed | tf_op | source)
XLA Modules:
  0.0 60.8 jit_solution(9692068732577621815)
XLA Ops:
  0.0 59.8 %shard_map.55 = bf16[120,4096]{1,0:T(8,128)(2,1)S(1)} custom-call(bf16[480,4096]{1,0:T(8,128)(2,1)} %bitcast.4, bf16[4096,512]{1,0:T(8,128)(2,1)} %interp_hbm.1, f32[64,512]{1,0:T(8,128)} %phases_ref.1, bf16[4,480,480]{2,1,0:T(8,128)(2,1)} %tables_hbm.1, s32[8,1,512]{2,1,0:T(1,128)} %bitcast.5), custom_call_target="tpu_custom_call" | custom-call | tf_op jit(solution)/shard_map/pallas_call | solution.py:239
  59.8 0.9 %copy.7 = bf16[4096,120]{0,1:T(8,128)(2,1)} copy(bf16[4096,120]{0,1:T(8,128)(2,1)S(1)} %bitcast.3) | data formatting | bytes 1966080
